TPU v7x, 32 devices: a whole 2x2x4 slice. The times are simulated.
32 devices in a mesh: seq: 8 (over z, x), head: 4 (over y, core).
Axes of the slice: x: 2, y: 2, z: 4, core: 2. Of those that a mesh axis runs over, the one named last changes fastest.
Arguments:
- queries: bfloat16 [2048, 2048], P('seq', 'head'), may hold values from -8 to 8
- keys: bfloat16 [2048, 512], P('seq', 'head'), may hold values from -4 to 4
- values: bfloat16 [2048, 512], P('seq', 'head'), may hold values from -6 to 6
- doc_ids: int32 [2048], replicated, may hold values from 0 to 15, never falling along the last dimension, each value on 1 to 1024 neighbouring positions
- span_order: int32 [16], replicated, may hold values from 0 to 15, each once
- out_weight: bfloat16 [2048, 4096], P('head', 'seq'), may hold values from -0.1875 to 0.1875
Outputs:
- layer_out: bfloat16 [2048, 4096], P('seq', 'head')
All inputs are finite; a program needn't handle non-finite values.
Results may differ from a plain program's by a relative error of at most 0.012.
Values may be sent and summed in bfloat16 or wider, within the bound.
A program may use at most 64 MiB of HBM per device.

v0:
```python
import functools
import math

import jax
import jax.numpy as jnp
from jax import lax
from jax.experimental import pallas as pl
from jax.experimental.pallas import tpu as pltpu
from jax.sharding import PartitionSpec as P

MESH = pl.DeviceIdType.MESH

DH = 128


def gathered_form(queries, keys, values, doc_ids, span_order, out_weight):
    tok_rows = queries.shape[0]
    span = tok_rows // 2
    local_heads = queries.shape[1] // DH
    local_kv = keys.shape[1] // DH
    group_size = local_heads // local_kv
    n_blocks = span_order.shape[0]
    scale = 1.0 / math.sqrt(DH)
    mine = lax.axis_index("seq")
    own_blocks = lax.dynamic_slice_in_dim(span_order, 2 * mine, 2, 0)
    local_rows = jnp.arange(tok_rows, dtype=jnp.int32)
    qpos = jnp.where(local_rows < span, own_blocks[0], own_blocks[1]) * span + local_rows % span
    qdoc = jnp.take(doc_ids, qpos)
    q_heads = queries.reshape(tok_rows, local_kv, group_size, DH)

    def update(state, kblk, vblk, kpos, kdoc):
        largest, total, summed = state
        count = kblk.shape[0]
        k_heads = kblk.reshape(count, local_kv, DH)
        v_heads = vblk.reshape(count, local_kv, DH)
        scores = (
            jnp.einsum("qhgd,khd->hgqk", q_heads, k_heads, preferred_element_type=jnp.float32)
            * scale
        )
        visible = (qdoc[:, None] == kdoc[None, :]) & (kpos[None, :] <= qpos[:, None])
        masked = jnp.where(visible, scores, jnp.float32(-1e30))
        new_largest = jnp.maximum(largest, jnp.max(masked, axis=-1))
        factor = jnp.exp(largest - new_largest)
        weights = jnp.where(visible, jnp.exp(masked - new_largest[..., None]), jnp.float32(0.0))
        total = total * factor + jnp.sum(weights, axis=-1)
        weights_b = weights.astype(jnp.bfloat16)
        added = jnp.einsum("hgqk,khd->qhgd", weights_b, v_heads, preferred_element_type=jnp.float32)
        summed = summed * jnp.transpose(factor, (2, 0, 1))[..., None] + added
        return (new_largest, total, summed)

    initial = (
        jnp.full((local_kv, group_size, tok_rows), -1e30, jnp.float32),
        jnp.zeros((local_kv, group_size, tok_rows), jnp.float32),
        jnp.zeros((tok_rows, local_kv, group_size, DH), jnp.float32),
    )
    state = initial
    kpiece = lax.all_gather(keys, "seq", axis=0, tiled=True)
    vpiece = lax.all_gather(values, "seq", axis=0, tiled=True)
    count = kpiece.shape[0]
    width = math.gcd(count, 1024)
    steps = count // width
    rows = jnp.arange(count, dtype=jnp.int32)
    match = (rows // span)[:, None] == jnp.arange(n_blocks, dtype=jnp.int32)[None, :]
    owner = jnp.sum(jnp.where(match, span_order[None, :], 0), axis=1)
    kpos = owner * span + rows % span
    kdoc = jnp.take(doc_ids, kpos)
    kparts = kpiece.reshape(steps, width, kpiece.shape[1])
    vparts = vpiece.reshape(steps, width, vpiece.shape[1])

    def one_step(carry, items):
        kblk, vblk, pblk, dblk = items
        carry = update(carry, kblk, vblk, pblk, dblk)
        return (carry, None)

    state, unused = lax.scan(
        one_step, state, (kparts, vparts, kpos.reshape(steps, width), kdoc.reshape(steps, width))
    )
    largest, total, summed = state
    attended = (summed / jnp.transpose(total, (2, 0, 1))[..., None]).astype(jnp.bfloat16)
    attended = attended.reshape(tok_rows, local_heads * DH)
    partial_out = jnp.dot(
        attended,
        lax.all_gather(out_weight, "seq", axis=1, tiled=True),
        preferred_element_type=jnp.float32,
    )
    return lax.psum_scatter(
        partial_out.astype(jnp.bfloat16), "head", scatter_dimension=1, tiled=True
    )


def ring_kernel(
    n, q_in, k_in, v_in, doc_in, order_in, w_in, out_ref,
    q_ref, doc_ref, order_ref, w_out, fetched, kbuf, vbuf, wbuf, bias, att, stage, kept, sums,
    k_send, k_recv, v_send, v_recv, w_send, w_recv, half_send, half_recv,
    att_send, att_recv, sum_send, sum_recv,
):
    seq = lax.axis_index("seq")
    head = lax.axis_index("head")
    pair, core = head // 2, head % 2
    partner = 2 * pair + 1 - core
    last = n // 2
    rows = q_ref.shape[0]
    span = rows // 2
    heads = q_ref.shape[1] // DH
    width = w_in.shape[1]
    half = width // 2
    quarter = half // 2
    pieces = (0, 2, 1, 3)
    scale = 1.0 / math.sqrt(DH)

    def seq_at(place):
        low = place // last
        return (1 - low) * 2 * place + low * (2 * (n - 1 - place) + 1)

    odd = seq % 2
    place = (1 - odd) * (seq // 2) + odd * (n - 1 - seq // 2)
    right, left = seq_at((place + 1) % n), seq_at((place + n - 1) % n)
    ring = ({"seq": right}, {"seq": left})

    def slot(way, dist):
        if dist == 0:
            return 0
        if dist == last:
            return n - 1
        return dist if way == 0 else last - 1 + dist

    def origin(number):
        if number < last:
            return seq_at((place + n - number) % n)
        if number == n - 1:
            return seq_at((place + last) % n)
        return seq_at((place + number - last + 1) % n)

    mine = pl.ds(pl.multiple_of(core * half, half), half)
    theirs = pl.ds(pl.multiple_of((1 - core) * half, half), half)
    fetches = [
        pltpu.make_async_copy(src, dst, fetched.at[at])
        for at, (src, dst) in enumerate(
            (
                (k_in, kbuf.at[0]),
                (v_in, vbuf.at[0]),
                (w_in.at[:, theirs], w_out),
                (w_in.at[:, mine], wbuf.at[0, 0]),
                (doc_in, doc_ref),
                (order_in, order_ref),
                (q_in, q_ref),
            )
        )
    ]
    for fetch in fetches:
        fetch.start()

    barrier = pltpu.get_barrier_semaphore()
    other = (pair + 1) % 2
    greet = ring + ({"head": partner}, {"head": 2 * other}, {"head": 2 * other + 1})
    for device in greet:
        pl.semaphore_signal(barrier, inc=1, device_id=device, device_id_type=MESH)
    pl.semaphore_wait(barrier, len(greet))

    sent = []

    def start(copy):
        copy.start()
        sent.append(copy)

    def remote(src, dst, send, recv, device):
        return pltpu.make_async_remote_copy(
            src_ref=src, dst_ref=dst, send_sem=send, recv_sem=recv, device_id=device, device_id_type=MESH
        )

    def kv_copy(which, way, dist):
        buf, ss, rs = ((kbuf, k_send, k_recv), (vbuf, v_send, v_recv))[which]
        to = slot(way, dist)
        return remote(buf.at[slot(way, dist - 1)], buf.at[to], ss.at[way, dist], rs.at[to], ring[way])

    def kv_goes(which, way, dist):
        return dist < last or (dist == last and which == way)

    def w_copy(way, dist, number):
        part, cut = number // 2, pl.ds(number % 2 * quarter, quarter)
        to = slot(way, dist)
        return remote(
            wbuf.at[slot(way, dist - 1), part, :, cut],
            wbuf.at[to, part, :, cut],
            w_send.at[way, dist, number],
            w_recv.at[to, number],
            ring[way],
        )

    def w_goes(way, dist, number):
        return dist < last or (dist == last and number // 2 == way)

    def half_copy(number):
        cut = pl.ds(number * quarter, quarter)
        return remote(
            w_out.at[:, cut], wbuf.at[0, 1, :, cut], half_send.at[number], half_recv.at[number], {"head": partner}
        )

    def send_kv(dist):
        for way in range(2):
            for which in range(2):
                if kv_goes(which, way, dist):
                    start(kv_copy(which, way, dist))

    def pass_kv(dist):
        for which in range(2):
            for way in range(2):
                if kv_goes(which, way, dist):
                    kv_copy(which, way, dist).wait_recv()
                    if kv_goes(which, way, dist + 1):
                        start(kv_copy(which, way, dist + 1))

    def send_w(dist, number):
        for way in range(2):
            if w_goes(way, dist, number):
                start(w_copy(way, dist, number))

    def pass_w(dist, number):
        for way in range(2):
            if w_goes(way, dist, number):
                w_copy(way, dist, number).wait_recv()
                if w_goes(way, dist + 1, number):
                    start(w_copy(way, dist + 1, number))

    fetches[0].wait()
    fetches[1].wait()
    send_kv(1)
    fetches[2].wait()
    for cut in range(2):
        start(half_copy(cut))
    fetches[3].wait()
    send_w(1, 0)
    for fetch in fetches[4:]:
        fetch.wait()

    down = lax.broadcasted_iota(jnp.int32, (span, span), 0)
    along = lax.broadcasted_iota(jnp.int32, (span, span), 1)
    query_at, query_doc = [], []
    for part in range(2):
        block = order_ref[2 * seq + part]
        query_at.append(down + block * span)
        docs = doc_ref[pl.ds(block, 1), :].astype(jnp.float32)
        query_doc.append(jnp.transpose(jnp.broadcast_to(docs, (span, span))))

    def mask(number):
        for j in range(2):
            block = order_ref[2 * origin(number) + j]
            docs = doc_ref[pl.ds(block, 1), :].astype(jnp.float32)
            key_at = along + block * span
            first = (2 * number + j) * span
            for part in range(2):
                seen = (query_doc[part] == docs) & (key_at <= query_at[part])
                bias[part, :, first : first + span] = jnp.where(seen, jnp.float32(0.0), jnp.float32(-1e30))

    mask(0)
    half_copy(0).wait_recv()
    send_w(1, 2)
    for dist in range(1, last + 1):
        pass_kv(dist)
        if dist == 1:
            send_w(1, 1)
        if dist == 2:
            half_copy(1).wait_recv()
            send_w(1, 3)
        if dist == last - 1:
            pass_w(1, pieces[0])
            pass_w(1, pieces[1])
        mask(slot(0, dist))
        if dist < last:
            mask(slot(1, dist))

    def attend(part, h):
        q = q_ref[part * span : (part + 1) * span, h * DH : (h + 1) * DH]
        keys = kbuf[...].reshape(n * rows, DH)
        scores = lax.dot_general(q, keys, (((1,), (1,)), ((), ())), preferred_element_type=jnp.float32)
        masked = scores * scale + bias[part]
        weights = jnp.exp(masked - jnp.max(masked, axis=-1, keepdims=True))
        total = jnp.sum(weights, axis=-1, keepdims=True)
        summed = jnp.dot(
            weights.astype(jnp.bfloat16), vbuf[...].reshape(n * rows, DH), preferred_element_type=jnp.float32
        )
        att[0, part * span : (part + 1) * span, h * DH : (h + 1) * DH] = (summed / total).astype(jnp.bfloat16)

    units = [(part, h) for part in range(2) for h in range(heads)]
    events = [(dist, number) for dist in range(1, last + 1) for number in pieces]
    cols_of = out_ref.shape[1] // width

    def target(number):
        block = origin(number)
        to = block // cols_of
        return block, to, 2 * ((pair + to // 2) % 2) + (core + to) % 2

    def sum_copy(number, cut):
        block, to, code = target(number)
        return remote(
            stage.at[number, cut],
            sums.at[code, block % cols_of, cut],
            sum_send.at[number, cut],
            sum_recv.at[code, block % cols_of, cut],
            {"head": to},
        )

    def project(number, cut):
        block, to, code = target(number)
        cols = slice(cut * quarter, (cut + 1) * quarter)
        added = jnp.dot(att[0], wbuf[number, 0, :, cols], preferred_element_type=jnp.float32)
        added = added + jnp.dot(att[1], wbuf[number, 1, :, cols], preferred_element_type=jnp.float32)

        @pl.when(code == 0)
        def _():
            kept[block % cols_of, cut] = added

        @pl.when(code != 0)
        def _():
            stage[number, cut] = added.astype(jnp.bfloat16)
            sum_copy(number, cut).start()

    def att_copy():
        return remote(att.at[0], att.at[1], att_send, att_recv, {"head": partner})

    ready = [(0, 0), (0, 1)]
    att_step = 0
    for at, (dist, number) in enumerate(events):
        if at > 1:
            pass_w(dist, number)
        if number >= 2:
            cut = number % 2
            ready += [(slot(0, dist), cut)] + ([(slot(1, dist), cut)] if dist < last else [])
        if at >= len(pieces) - 1:
            for part, h in units[:2]:
                attend(part, h)
            units = units[2:]
        if not units:
            att_step += 1
            if att_step == 1:
                start(att_copy())
            if att_step == 2:
                att_copy().wait_recv()
        if att_step > 1:
            for _ in range(4):
                if ready:
                    project(*ready.pop(0))
    for item in ready:
        project(*item)

    own = pl.multiple_of(core * half, half)
    far = pl.multiple_of((1 - core) * half, half)
    for cut in range(2):
        for j in range(cols_of):
            for code in range(1, 4):
                remote(
                    stage.at[0, cut], sums.at[code, j, cut], sum_send.at[0, cut], sum_recv.at[code, j, cut], {"head": partner}
                ).wait_recv()
            at = j * width + cut * quarter
            out_ref[:, pl.ds(pl.multiple_of(at + own, quarter), quarter)] = (
                kept[j, cut] + sums[2, j, cut].astype(jnp.float32)
            ).astype(jnp.bfloat16)
            out_ref[:, pl.ds(pl.multiple_of(at + far, quarter), quarter)] = (
                sums[1, j, cut].astype(jnp.float32) + sums[3, j, cut].astype(jnp.float32)
            ).astype(jnp.bfloat16)
    for copy in sent:
        copy.wait_send()
    for number in range(n):

        @pl.when(target(number)[2] != 0)
        def _(number=number):
            for cut in range(2):
                sum_copy(number, cut).wait_send()


def ring_form(n, queries, keys, values, doc_ids, span_order, out_weight):
    rows = queries.shape[0]
    depth, width = out_weight.shape
    half = width // 2
    per_head = n // 4
    bf16 = jnp.bfloat16
    dma = pltpu.SemaphoreType.DMA
    return pl.pallas_call(
        functools.partial(ring_kernel, n),
        out_shape=jax.ShapeDtypeStruct((rows, width * per_head), bf16),
        in_specs=[pl.BlockSpec(memory_space=pl.ANY)] * 6,
        out_specs=pl.BlockSpec(memory_space=pltpu.VMEM),
        scratch_shapes=[
            pltpu.VMEM(queries.shape, bf16),
            pltpu.VMEM((doc_ids.shape[0] // (rows // 2), rows // 2), jnp.int32),
            pltpu.SMEM(span_order.shape, jnp.int32),
            pltpu.VMEM((depth, half), bf16),
            dma((7,)),
            pltpu.VMEM((n, rows, DH), bf16),
            pltpu.VMEM((n, rows, DH), bf16),
            pltpu.VMEM((n, 2, depth, half), bf16),
            pltpu.VMEM((2, rows // 2, n * rows), jnp.float32),
            pltpu.VMEM((2,) + queries.shape, bf16),
            pltpu.VMEM((n, 2, rows, half // 2), bf16),
            pltpu.VMEM((per_head, 2, rows, half // 2), jnp.float32),
            pltpu.VMEM((4, per_head, 2, rows, half // 2), bf16),
            dma((2, n // 2 + 1)),
            dma((n,)),
            dma((2, n // 2 + 1)),
            dma((n,)),
            dma((2, n // 2 + 1, 4)),
            dma((n, 4)),
            dma((2,)),
            dma((2,)),
            dma,
            dma,
            dma((n, 2)),
            dma((4, per_head, 2)),
        ],
        compiler_params=pltpu.CompilerParams(
            collective_id=0, has_side_effects=True, vmem_limit_bytes=62 * 1024 * 1024
        ),
    )(queries, keys, values, doc_ids.reshape(-1, rows // 2), span_order, out_weight)


def on_device(mesh_shape, queries, keys, values, doc_ids, span_order, out_weight):
    n, groups = mesh_shape["seq"], mesh_shape["head"]
    rows = queries.shape[0]
    depth, width = out_weight.shape
    held = n * (depth * width + 2 * rows * DH) * 2
    fits = (
        groups == 4
        and n % 4 == 0
        and rows == 2 * DH
        and keys.shape[1] == DH
        and width % (4 * DH) == 0
        and held <= 16 * 1024 * 1024
    )
    if fits:
        return ring_form(n, queries, keys, values, doc_ids, span_order, out_weight)
    return gathered_form(queries, keys, values, doc_ids, span_order, out_weight)


def solution(mesh):
    return jax.shard_map(
        functools.partial(on_device, dict(mesh.shape)),
        mesh=mesh,
        in_specs=(P("seq", "head"), P("seq", "head"), P("seq", "head"), P(), P(), P("head", "seq")),
        out_specs=P("seq", "head"),
        check_vma=False,
    )
```

profile of v0, /device:TPU:0, one launch (start us, length us, event | category | flops | bytes accessed | tf_op | source)
XLA Modules:
  0.0 61.0 jit_solution(4891361602595919071)
XLA Ops:
  0.0 59.1 %shard_map.64 = bf16[256,1024]{1,0:T(8,128)(2,1)} custom-call(bf16[256,512]{1,0:T(8,128)(2,1)} %q_in.1, bf16[256,128]{1,0:T(8,128)(2,1)} %k_in.1, bf16[256,128]{1,0:T(8,128)(2,1)} %v_in.1, s32[16,128]{1,0:T(8,128)} %bitcast.1, s32[16]{0:T(128)} %order_in.1, bf16[512,512]{1,0:T(8,128)(2,1)} %w_in.1), custom_call_target="tpu_custom_call" | custom-call | tf_op jit(solution)/shard_map/pallas_call | solution.py:378
  59.1 1.9 %copy.8 = bf16[256,1024]{1,0:T(8,128)(2,1)} copy(bf16[256,1024]{1,0:T(8,128)(2,1)} %shard_map.64) | data formatting | bytes 1048576
where the time goes:
time: 61.1 us; the launch traced here: 61 us
  Pallas kernels  59.1 us (97%)
  local copies, waits for them, and re-layouts  1.87 us (3%)
    pallas_call x1, Pallas kernels, ring_form(): pl.pallas_call(functools.partial(ring_kernel, n), out_shape=jax.ShapeDtyp...  59.1 us
    unnamed x1, local copies, waits for them, and re-layouts  1.87 us

commit v1 on v0

v1 whole, which is shorter than its diff:
```python
import functools
import math

import jax
import jax.numpy as jnp
from jax import lax
from jax.experimental import pallas as pl
from jax.experimental.pallas import tpu as pltpu
from jax.sharding import PartitionSpec as P

MESH = pl.DeviceIdType.MESH

DH = 128
NEG = -1e30

def gathered_form(queries, keys, values, doc_ids, span_order, out_weight):
    tok_rows = queries.shape[0]
    span = tok_rows // 2
    local_heads = queries.shape[1] // DH
    local_kv = keys.shape[1] // DH
    group_size = local_heads // local_kv
    n_blocks = span_order.shape[0]
    scale = 1.0 / math.sqrt(DH)
    mine = lax.axis_index("seq")
    own_blocks = lax.dynamic_slice_in_dim(span_order, 2 * mine, 2, 0)
    local_rows = jnp.arange(tok_rows, dtype=jnp.int32)
    qpos = jnp.where(local_rows < span, own_blocks[0], own_blocks[1]) * span + local_rows % span
    qdoc = jnp.take(doc_ids, qpos)
    q_heads = queries.reshape(tok_rows, local_kv, group_size, DH)

    def update(state, kblk, vblk, kpos, kdoc):
        largest, total, summed = state
        count = kblk.shape[0]
        k_heads = kblk.reshape(count, local_kv, DH)
        v_heads = vblk.reshape(count, local_kv, DH)
        scores = (
            jnp.einsum("qhgd,khd->hgqk", q_heads, k_heads, preferred_element_type=jnp.float32)
            * scale
        )
        visible = (qdoc[:, None] == kdoc[None, :]) & (kpos[None, :] <= qpos[:, None])
        masked = jnp.where(visible, scores, jnp.float32(-1e30))
        new_largest = jnp.maximum(largest, jnp.max(masked, axis=-1))
        factor = jnp.exp(largest - new_largest)
        weights = jnp.where(visible, jnp.exp(masked - new_largest[..., None]), jnp.float32(0.0))
        total = total * factor + jnp.sum(weights, axis=-1)
        weights_b = weights.astype(jnp.bfloat16)
        added = jnp.einsum("hgqk,khd->qhgd", weights_b, v_heads, preferred_element_type=jnp.float32)
        summed = summed * jnp.transpose(factor, (2, 0, 1))[..., None] + added
        return (new_largest, total, summed)

    initial = (
        jnp.full((local_kv, group_size, tok_rows), -1e30, jnp.float32),
        jnp.zeros((local_kv, group_size, tok_rows), jnp.float32),
        jnp.zeros((tok_rows, local_kv, group_size, DH), jnp.float32),
    )
    state = initial
    kpiece = lax.all_gather(keys, "seq", axis=0, tiled=True)
    vpiece = lax.all_gather(values, "seq", axis=0, tiled=True)
    count = kpiece.shape[0]
    width = math.gcd(count, 1024)
    steps = count // width
    rows = jnp.arange(count, dtype=jnp.int32)
    match = (rows // span)[:, None] == jnp.arange(n_blocks, dtype=jnp.int32)[None, :]
    owner = jnp.sum(jnp.where(match, span_order[None, :], 0), axis=1)
    kpos = owner * span + rows % span
    kdoc = jnp.take(doc_ids, kpos)
    kparts = kpiece.reshape(steps, width, kpiece.shape[1])
    vparts = vpiece.reshape(steps, width, vpiece.shape[1])

    def one_step(carry, items):
        kblk, vblk, pblk, dblk = items
        carry = update(carry, kblk, vblk, pblk, dblk)
        return (carry, None)

    state, unused = lax.scan(
        one_step, state, (kparts, vparts, kpos.reshape(steps, width), kdoc.reshape(steps, width))
    )
    largest, total, summed = state
    attended = (summed / jnp.transpose(total, (2, 0, 1))[..., None]).astype(jnp.bfloat16)
    attended = attended.reshape(tok_rows, local_heads * DH)
    partial_out = jnp.dot(
        attended,
        lax.all_gather(out_weight, "seq", axis=1, tiled=True),
        preferred_element_type=jnp.float32,
    )
    return lax.psum_scatter(
        partial_out.astype(jnp.bfloat16), "head", scatter_dimension=1, tiled=True
    )


def line_kernel(
    n, q_in, k_in, v_in, doc_in, order_in, w_in, out_ref,
    q_ref, doc_ref, order_ref, fetched, kbuf, vbuf, wbuf, bias, best, acc, att, far, stage, sums,
    kv_send, kv_recv, w_send, w_recv, att_send, att_recv, far_send, far_recv, sum_send, sum_recv,
):
    seq, head = lax.axis_index("seq"), lax.axis_index("head")
    z, x, y, c = seq // 2, seq % 2, head // 2, head % 2
    side = z // 2
    role = (z + side) % 2
    rows = q_ref.shape[0]
    span = rows // 2
    heads = q_ref.shape[1] // DH
    depth, width = w_in.shape
    half, deep = width // 2, depth // 2
    factor = math.log2(math.e) / math.sqrt(DH)
    slabs = n // 2
    far_slab = slabs - 1
    cuts = range(2)
    parts = [(cut, low) for cut in range(2) for low in range(2)]

    def slab(k):
        return k + side * (slabs - 1 - 2 * k)

    def place(zz, xx, yy, cc):
        return {"seq": 2 * zz + xx, "head": 2 * yy + cc}

    inward = place((1 - role) * slab(1) + role * slab(2), x, y, c)
    outward = place(slab(0), x, y, c)
    across = {"seq": 2 * z + 1 - x}
    partner = {"head": 2 * y + 1 - c}
    ways = (inward, outward, across)

    own = role
    fetches = [
        pltpu.make_async_copy(src, dst, fetched.at[at])
        for at, (src, dst) in enumerate(
            [(k_in, kbuf.at[own, 0]), (v_in, vbuf.at[own, 0])]
            + [
                (w_in.at[pl.ds(low * deep, deep), pl.ds(cut * half, half)], wbuf.at[own, cut, pl.ds(low * deep, deep)])
                for cut, low in parts
            ]
            + [(doc_in, doc_ref), (order_in, order_ref), (q_in, q_ref)]
        )
    ]
    for fetch in fetches:
        fetch.start()

    barrier = pltpu.get_barrier_semaphore()
    for zz in range(2):
        for flip in range(8):
            fx, fy, fc = flip // 4, flip // 2 % 2, flip % 2
            if zz or flip:
                there = place((z - 2 * side + zz) % 2 + 2 * side, (x + fx) % 2, (y + fy) % 2, (c + fc) % 2)
                pl.semaphore_signal(barrier, inc=1, device_id=there, device_id_type=MESH)

    @pl.when(role == 1)
    def _():
        pl.semaphore_signal(barrier, inc=1, device_id=inward, device_id_type=MESH)

    pl.semaphore_wait(barrier, 15 + role)

    def remote(src, dst, send, recv, device):
        return pltpu.make_async_remote_copy(
            src_ref=src, dst_ref=dst, send_sem=send, recv_sem=recv, device_id=device, device_id_type=MESH
        )

    sent = ([], [])

    def go(who, make):
        make().start()
        sent[who].append(make)

    def arrive(dst, recv):
        remote(dst, dst, att_send.at[0], recv, partner).wait_recv()

    def kv_send_to(who, which, way, k):
        buf = (kbuf, vbuf)[which]
        to = slabs - 1 - k if (who == 1 and way == 0) else k
        lane = 1 if way == 2 else 0
        go(
            who,
            lambda: remote(
                buf.at[k, 0], buf.at[to, lane], kv_send.at[which, way, k], kv_recv.at[which, lane, to], ways[way]
            ),
        )

    def kv_wait(which, lane, k):
        arrive((kbuf, vbuf)[which].at[k, lane], kv_recv.at[which, lane, k])

    def w_at(k, cut, low, mine):
        return wbuf.at[k, cut, pl.ds(mine * depth + low * deep, deep)]

    def w_send_to(who, way, k, cut, low):
        to = slabs - 1 - k if (who == 1 and way == 0) else k
        mine = 1 if way == 2 else 0
        go(
            who,
            lambda: remote(
                w_at(k, cut, low, 0), w_at(to, cut, low, mine), w_send.at[way, k, cut, low],
                w_recv.at[mine, to, cut, low], partner if way == 2 else ways[way],
            ),
        )

    def w_wait(mine, k, cut, low):
        arrive(w_at(k, cut, low, mine), w_recv.at[mine, k, cut, low])

    def each(end, middle):
        @pl.when(role == 0)
        def _():
            end(0)

        @pl.when(role == 1)
        def _():
            middle(1)

    for which in range(2):
        fetches[which].wait()

        def end(who):
            for way in (0, 2):
                kv_send_to(who, which, way, 0)

        def middle(who):
            for way in (1, 0, 2):
                kv_send_to(who, which, way, 1)

        each(end, middle)
    for fetch in fetches[2:]:
        fetch.wait()

    def end(who):
        for cut, low in parts:
            w_send_to(who, 0, 0, cut, low)
        for cut, low in parts:
            w_send_to(who, 2, 0, cut, low)

    def middle(who):
        for cut, low in parts:
            w_send_to(who, 2, 1, cut, low)

    each(end, middle)

    down = lax.broadcasted_iota(jnp.int32, (span, span), 0)
    along = lax.broadcasted_iota(jnp.int32, (span, span), 1)
    query_at, query_doc = [], []
    for part in range(2):
        block = order_ref[2 * seq + part]
        query_at.append(down + block * span)
        docs = doc_ref[pl.ds(block, 1), :].astype(jnp.float32)
        query_doc.append(jnp.transpose(jnp.broadcast_to(docs, (span, span))))

    order = (role, 1 - role, 2, 3)

    def mask(step):
        for lane in range(2):
            source = 2 * slab(order[step]) + (x if lane == 0 else 1 - x)
            for j in range(2):
                block = order_ref[2 * source + j]
                docs = doc_ref[pl.ds(block, 1), :].astype(jnp.float32)
                key_at = along + block * span
                first = (2 * lane + j) * span
                for part in range(2):
                    seen = (query_doc[part] == docs) & (key_at <= query_at[part])
                    bias[step % 2, part * span : (part + 1) * span, first : first + span] = jnp.where(
                        seen, jnp.float32(0.0), jnp.float32(NEG)
                    )

    def attend(step, h):
        k = order[step]
        count = 2 * rows
        q = q_ref[:, h * DH : (h + 1) * DH]
        scores = lax.dot_general(
            q, kbuf[k].reshape(count, DH), (((1,), (1,)), ((), ())), preferred_element_type=jnp.float32
        )
        masked = scores * factor + bias[step % 2]
        top = jnp.broadcast_to(jnp.max(masked, axis=-1, keepdims=True), (rows, DH))
        if step > 0:
            before = best[h]
            top = jnp.maximum(before, top)
        weights = jnp.concatenate(
            [jnp.exp2(masked[:, at : at + DH] - top).astype(jnp.bfloat16) for at in range(0, count, DH)], axis=1
        )
        wide = jnp.concatenate([vbuf[k].reshape(count, DH), jnp.ones((count, DH), jnp.bfloat16)], axis=1)
        summed = jnp.dot(weights, wide, preferred_element_type=jnp.float32)
        if step > 0:
            fade = jnp.exp2(before - top)
            summed = summed + acc[h] * jnp.concatenate([fade, fade], axis=1)
        if step < slabs - 1:
            best[h] = top
            acc[h] = summed
        else:
            att[2, :, h * DH : (h + 1) * DH] = (summed[:, :DH] / summed[:, DH:]).astype(jnp.bfloat16)

    def group(step):
        for which in range(2):
            kv_wait(which, 1, order[step])
        for h in range(heads):
            attend(step, h)

    mask(0)

    def end(who):
        for which in range(2):
            kv_wait(which, 0, 1)
            kv_send_to(who, which, 2, 1)

    def middle(who):
        for which in range(2):
            kv_wait(which, 0, 0)
            kv_send_to(who, which, 0, 0)
            kv_send_to(who, which, 2, 0)
            kv_wait(which, 0, 2)
            kv_send_to(who, which, 1, 2)
            kv_send_to(who, which, 2, 2)
        for cut, low in parts:
            w_send_to(who, 0, 1, cut, low)

    each(end, middle)
    mask(1)
    group(0)

    def end(who):
        for which in range(2):
            kv_wait(which, 0, 2)
            kv_send_to(who, which, 2, 2)

    def middle(who):
        for which in range(2):
            kv_wait(which, 0, 3)
            kv_send_to(who, which, 1, 3)
            kv_send_to(who, which, 2, 3)
        for cut, low in parts:
            w_send_to(who, 1, 1, cut, low)

    each(end, middle)
    group(1)
    mask(2)
    mask(3)

    def end(who):
        for which in range(2):
            kv_wait(which, 0, 3)
            kv_send_to(who, which, 2, 3)

    each(end, lambda who: None)
    group(2)
    group(3)

    cross = place(z, 1 - x, y, x)
    own_rows = c == x
    cross_part = (c + x) % 2
    first_part = 2 * (1 - cross_part)

    def att_cross():
        return remote(att.at[2], att.at[cross_part], att_send.at[0], att_recv.at[cross_part], cross)

    def att_near():
        return remote(att.at[2], att.at[1], att_send.at[1], att_recv.at[1], partner)

    att_cross().start()

    @pl.when(jnp.logical_not(own_rows))
    def _():
        att_near().start()

    def pass_w(who, k, which, way):
        for cut, low in which:
            w_wait(0, k, cut, low)
            if way is not None:
                w_send_to(who, way, k, cut, low)
            w_send_to(who, 2, k, cut, low)

    def att_wait():
        arrive(att.at[1], att_recv.at[1])

        @pl.when(jnp.logical_not(own_rows))
        def _():
            arrive(att.at[0], att_recv.at[0])

    def end(who):
        pass_w(who, 1, parts[:2], None)

    def middle(who):
        pass_w(who, 0, parts[:2], 0)
        pass_w(who, 2, parts[:1], 1)
        pass_w(who, 0, parts[2:], 0)
        pass_w(who, 2, parts[1:], 1)

    each(end, middle)
    att_wait()

    def far_copy(part):
        src = first_part if part == 0 else 1
        return remote(att.at[src], far.at[part], far_send.at[part], far_recv.at[part], inward)

    def end(who):
        for part in range(2):
            go(who, functools.partial(far_copy, part))

    each(end, lambda who: None)

    def sum_copy(k, slot, cut, zz):
        return remote(
            stage.at[slot, cut], sums.at[y, x, cut], sum_send.at[slot, cut], sum_recv.at[y, x, cut],
            {"seq": 2 * zz + c, "head": slab(k)},
        )

    def here(k):
        return own_rows & (slab(k) == head)

    def product(k, cut, first, second):
        added = jnp.dot(first, wbuf[k, cut, :depth, :], preferred_element_type=jnp.float32)
        return added + jnp.dot(second, wbuf[k, cut, depth:, :], preferred_element_type=jnp.float32)

    def project(k, slot, cut):
        value = product(k, cut, att[first_part], att[1]).astype(jnp.bfloat16)

        @pl.when(here(k))
        def _():
            sums[y, x, cut] = value

        @pl.when(jnp.logical_not(here(k)))
        def _():
            stage[slot, cut] = value
            sum_copy(k, slot, cut, z).start()

    def project_far(who, cut):
        stage[slabs, cut] = product(far_slab, cut, far[0], far[1]).astype(jnp.bfloat16)
        go(who, lambda: sum_copy(far_slab, slabs, cut, slab(0)))

    def near_w(k, cut):
        for low in range(2):
            w_wait(1, k, cut, low)

    for cut in cuts:
        near_w(order[0], cut)
        project(order[0], 0, cut)

    def end(who):
        pass_w(who, 1, parts[2:], None)

    each(end, lambda who: None)
    for cut in cuts:
        near_w(order[1], cut)
        project(order[1], 1, cut)
    for cut in cuts:

        def end(who):
            pass_w(who, 2, [(cut, low) for low in range(2)], None)

        each(end, lambda who: None)
        near_w(2, cut)
        project(2, 2, cut)

    def middle(who):
        for cut in cuts:
            pass_w(who, 3, [(cut, low) for low in range(2)], None)
            near_w(3, cut)
            if cut == 0:
                for part in range(2):
                    arrive(far.at[part], far_recv.at[part])
            project_far(who, cut)
            project(3, 3, cut)

    each(lambda who: None, middle)

    stays = own_rows & ((role == 1) | (slab(far_slab) != head))
    for cut in cuts:
        for lane in range(2):
            for row in range(2):

                @pl.when(jnp.logical_not(stays & (row == y) & (lane == x)))
                def _():
                    arrive(sums.at[row, lane, cut], sum_recv.at[row, lane, cut])

            at = lane * width + cut * half
            out_ref[:, at : at + half] = (
                sums[0, lane, cut].astype(jnp.float32) + sums[1, lane, cut].astype(jnp.float32)
            ).astype(jnp.bfloat16)

    def finish(who):
        for make in sent[who]:
            make().wait_send()

    each(finish, finish)
    att_cross().wait_send()

    @pl.when(jnp.logical_not(own_rows))
    def _():
        att_near().wait_send()

    for step in range(slabs):
        k = order[step]
        made = jnp.logical_not(here(k))
        if step == far_slab:
            made = made & (role == 1)

        @pl.when(made)
        def _(k=k, step=step):
            for cut in cuts:
                sum_copy(k, step, cut, z).wait_send()


def line_form(n, queries, keys, values, doc_ids, span_order, out_weight):
    rows = queries.shape[0]
    depth, width = out_weight.shape
    half = width // 2
    slabs = n // 2
    heads = queries.shape[1] // DH
    bf16 = jnp.bfloat16
    dma = pltpu.SemaphoreType.DMA
    return pl.pallas_call(
        functools.partial(line_kernel, n),
        out_shape=jax.ShapeDtypeStruct((rows, 2 * width), bf16),
        in_specs=[pl.BlockSpec(memory_space=pl.ANY)] * 6,
        out_specs=pl.BlockSpec(memory_space=pltpu.VMEM),
        scratch_shapes=[
            pltpu.VMEM(queries.shape, bf16),
            pltpu.VMEM((doc_ids.shape[0] // (rows // 2), rows // 2), jnp.int32),
            pltpu.SMEM(span_order.shape, jnp.int32),
            dma((9,)),
            pltpu.VMEM((slabs, 2, rows, DH), bf16),
            pltpu.VMEM((slabs, 2, rows, DH), bf16),
            pltpu.VMEM((slabs, 2, 2 * depth, half), bf16),
            pltpu.VMEM((2, rows, 2 * rows), jnp.float32),
            pltpu.VMEM((heads, rows, DH), jnp.float32),
            pltpu.VMEM((heads, rows, 2 * DH), jnp.float32),
            pltpu.VMEM((3,) + queries.shape, bf16),
            pltpu.VMEM((2,) + queries.shape, bf16),
            pltpu.VMEM((slabs + 1, 2, rows, half), bf16),
            pltpu.VMEM((2, 2, 2, rows, half), bf16),
            dma((2, 3, slabs)),
            dma((2, 2, slabs)),
            dma((3, slabs, 2, 2)),
            dma((2, slabs, 2, 2)),
            dma((2,)),
            dma((2,)),
            dma((2,)),
            dma((2,)),
            dma((slabs + 1, 2)),
            dma((2, 2, 2)),
        ],
        compiler_params=pltpu.CompilerParams(
            collective_id=0, has_side_effects=True, vmem_limit_bytes=62 * 1024 * 1024
        ),
    )(queries, keys, values, doc_ids.reshape(-1, rows // 2), span_order, out_weight)


def on_device(mesh_shape, queries, keys, values, doc_ids, span_order, out_weight):
    n, groups = mesh_shape["seq"], mesh_shape["head"]
    rows = queries.shape[0]
    depth, width = out_weight.shape
    fits = (
        groups == 4
        and n == 2 * groups
        and rows == 2 * DH
        and keys.shape[1] == DH
        and queries.shape[1] == depth
        and depth % (2 * DH) == 0
        and width % (4 * DH) == 0
        and depth * width <= 512 * 512
    )
    if fits:
        return line_form(n, queries, keys, values, doc_ids, span_order, out_weight)
    return gathered_form(queries, keys, values, doc_ids, span_order, out_weight)


def solution(mesh):
    return jax.shard_map(
        functools.partial(on_device, dict(mesh.shape)),
        mesh=mesh,
        in_specs=(P("seq", "head"), P("seq", "head"), P("seq", "head"), P(), P(), P("head", "seq")),
        out_specs=P("seq", "head"),
        check_vma=False,
    )
```

time: 61.1 us -> 52.7 us (0.86)
  Pallas kernels: 59.1 us -> 50.7 us
    pallas_call x1, Pallas kernels: 59.1 us -> 50.7 us  [line_form(): pl.pallas_call(functools.partial(line_kernel, n), out_shape=jax.ShapeDtyp...]
where the time goes in v1:
time: 52.7 us; the launch traced here: 52.6 us
  Pallas kernels  50.7 us (96%)
  local copies, waits for them, and re-layouts  1.87 us (4%)
    pallas_call x1, Pallas kernels, line_form(): pl.pallas_call(functools.partial(line_kernel, n), out_shape=jax.ShapeDtyp...  50.7 us
    unnamed x1, local copies, waits for them, and re-layouts  1.87 us

profile of v1, /device:TPU:0, one launch (start us, length us, event | category | flops | bytes accessed | tf_op | source)
XLA Modules:
  0.0 52.6 jit_solution(3824079621945974673)
XLA Ops:
  0.0 50.7 %shard_map.64 = bf16[256,1024]{1,0:T(8,128)(2,1)} custom-call(bf16[256,512]{1,0:T(8,128)(2,1)} %q_in.1, bf16[256,128]{1,0:T(8,128)(2,1)} %k_in.1, bf16[256,128]{1,0:T(8,128)(2,1)} %v_in.1, s32[16,128]{1,0:T(8,128)} %bitcast.1, s32[16]{0:T(128)} %order_in.1, bf16[512,512]{1,0:T(8,128)(2,1)} %w_in.1), custom_call_target="tpu_custom_call" | custom-call | tf_op jit(solution)/shard_map/pallas_call | solution.py:502
  50.7 1.9 %copy.8 = bf16[256,1024]{1,0:T(8,128)(2,1)} copy(bf16[256,1024]{1,0:T(8,128)(2,1)} %shard_map.64) | data formatting | bytes 1048576

commit v2 on v1

--- a/solution.py
+++ b/solution.py
@@ -218,17 +218,6 @@
     for fetch in fetches[2:]:
         fetch.wait()
 
-    def end(who):
-        for cut, low in parts:
-            w_send_to(who, 0, 0, cut, low)
-        for cut, low in parts:
-            w_send_to(who, 2, 0, cut, low)
-
-    def middle(who):
-        for cut, low in parts:
-            w_send_to(who, 2, 1, cut, low)
-
-    each(end, middle)
 
     down = lax.broadcasted_iota(jnp.int32, (span, span), 0)
     along = lax.broadcasted_iota(jnp.int32, (span, span), 1)
@@ -293,6 +282,10 @@
         for which in range(2):
             kv_wait(which, 0, 1)
             kv_send_to(who, which, 2, 1)
+        for cut, low in parts:
+            w_send_to(who, 0, 0, cut, low)
+        for cut, low in parts:
+            w_send_to(who, 2, 0, cut, low)
 
     def middle(who):
         for which in range(2):
@@ -304,6 +297,14 @@
             kv_send_to(who, which, 2, 2)
         for cut, low in parts:
             w_send_to(who, 0, 1, cut, low)
+        for which in range(2):
+            kv_wait(which, 0, 3)
+            kv_send_to(who, which, 1, 3)
+            kv_send_to(who, which, 2, 3)
+        for cut, low in parts[:2]:
+            w_send_to(who, 1, 1, cut, low)
+        for cut, low in parts:
+            w_send_to(who, 2, 1, cut, low)
 
     each(end, middle)
     mask(1)
@@ -314,44 +315,10 @@
             kv_wait(which, 0, 2)
             kv_send_to(who, which, 2, 2)
 
-    def middle(who):
-        for which in range(2):
-            kv_wait(which, 0, 3)
-            kv_send_to(who, which, 1, 3)
-            kv_send_to(who, which, 2, 3)
-        for cut, low in parts:
-            w_send_to(who, 1, 1, cut, low)
-
-    each(end, middle)
+    each(end, lambda who: None)
     group(1)
     mask(2)
     mask(3)
-
-    def end(who):
-        for which in range(2):
-            kv_wait(which, 0, 3)
-            kv_send_to(who, which, 2, 3)
-
-    each(end, lambda who: None)
-    group(2)
-    group(3)
-
-    cross = place(z, 1 - x, y, x)
-    own_rows = c == x
-    cross_part = (c + x) % 2
-    first_part = 2 * (1 - cross_part)
-
-    def att_cross():
-        return remote(att.at[2], att.at[cross_part], att_send.at[0], att_recv.at[cross_part], cross)
-
-    def att_near():
-        return remote(att.at[2], att.at[1], att_send.at[1], att_recv.at[1], partner)
-
-    att_cross().start()
-
-    @pl.when(jnp.logical_not(own_rows))
-    def _():
-        att_near().start()
 
     def pass_w(who, k, which, way):
         for cut, low in which:
@@ -360,6 +327,41 @@
                 w_send_to(who, way, k, cut, low)
             w_send_to(who, 2, k, cut, low)
 
+    def end(who):
+        for which in range(2):
+            kv_wait(which, 0, 3)
+            kv_send_to(who, which, 2, 3)
+
+    def middle(who):
+        pass_w(who, 2, parts[:1], 1)
+
+    each(end, middle)
+    group(2)
+
+    def middle(who):
+        pass_w(who, 0, parts[:2], 0)
+        pass_w(who, 2, parts[1:2], 1)
+
+    each(lambda who: None, middle)
+    group(3)
+
+    cross = place(z, 1 - x, y, x)
+    own_rows = c == x
+    cross_part = (c + x) % 2
+    first_part = 2 * (1 - cross_part)
+
+    def att_cross():
+        return remote(att.at[2], att.at[cross_part], att_send.at[0], att_recv.at[cross_part], cross)
+
+    def att_near():
+        return remote(att.at[2], att.at[1], att_send.at[1], att_recv.at[1], partner)
+
+    att_cross().start()
+
+    @pl.when(jnp.logical_not(own_rows))
+    def _():
+        att_near().start()
+
     def att_wait():
         arrive(att.at[1], att_recv.at[1])
 
@@ -371,10 +373,10 @@
         pass_w(who, 1, parts[:2], None)
 
     def middle(who):
-        pass_w(who, 0, parts[:2], 0)
-        pass_w(who, 2, parts[:1], 1)
         pass_w(who, 0, parts[2:], 0)
-        pass_w(who, 2, parts[1:], 1)
+        pass_w(who, 2, parts[2:], 1)
+        for cut, low in parts[2:]:
+            w_send_to(who, 1, 1, cut, low)
 
     each(end, middle)
     att_wait()
@@ -426,13 +428,14 @@
         near_w(order[0], cut)
         project(order[0], 0, cut)
 
-    def end(who):
-        pass_w(who, 1, parts[2:], None)
-
-    each(end, lambda who: None)
-    for cut in cuts:
-        near_w(order[1], cut)
-        project(order[1], 1, cut)
+    near_w(order[1], 0)
+    project(order[1], 1, 0)
+
+    def middle(who):
+        near_w(0, 1)
+        project(0, 1, 1)
+
+    each(lambda who: None, middle)
     for cut in cuts:
 
         def end(who):
@@ -442,17 +445,24 @@
         near_w(2, cut)
         project(2, 2, cut)
 
+    def end(who):
+        pass_w(who, 1, parts[2:], None)
+        near_w(1, 1)
+        project(1, 1, 1)
+
     def middle(who):
-        for cut in cuts:
-            pass_w(who, 3, [(cut, low) for low in range(2)], None)
-            near_w(3, cut)
-            if cut == 0:
-                for part in range(2):
-                    arrive(far.at[part], far_recv.at[part])
-            project_far(who, cut)
-            project(3, 3, cut)
-
-    each(lambda who: None, middle)
+        pass_w(who, 3, parts[:2], None)
+        near_w(3, 0)
+        project(3, 3, 0)
+        pass_w(who, 3, parts[2:], None)
+        for part in range(2):
+            arrive(far.at[part], far_recv.at[part])
+        project_far(who, 0)
+        near_w(3, 1)
+        project_far(who, 1)
+        project(3, 3, 1)
+
+    each(end, middle)
 
     stays = own_rows & ((role == 1) | (slab(far_slab) != head))
     for cut in cuts:

time: 52.7 us -> 50.4 us (0.956)
  Pallas kernels: 50.7 us -> 47.9 us
    pallas_call x1, Pallas kernels: 50.7 us -> 47.9 us  [line_form(): pl.pallas_call(functools.partial(line_kernel, n), out_shape=jax.ShapeDtyp...]
where the time goes in v2:
time: 50.4 us; the launch traced here: 49.7 us
  Pallas kernels  47.9 us (95%)
  local copies, waits for them, and re-layouts  1.87 us (4%)
    pallas_call x1, Pallas kernels, line_form(): pl.pallas_call(functools.partial(line_kernel, n), out_shape=jax.ShapeDtyp...  47.9 us
    unnamed x1, local copies, waits for them, and re-layouts  1.87 us

profile of v2, /device:TPU:0, one launch (start us, length us, event | category | flops | bytes accessed | tf_op | source)
XLA Modules:
  0.0 49.7 jit_solution(3269546126864243481)
XLA Ops:
  0.0 47.9 %shard_map.64 = bf16[256,1024]{1,0:T(8,128)(2,1)} custom-call(bf16[256,512]{1,0:T(8,128)(2,1)} %q_in.1, bf16[256,128]{1,0:T(8,128)(2,1)} %k_in.1, bf16[256,128]{1,0:T(8,128)(2,1)} %v_in.1, s32[16,128]{1,0:T(8,128)} %bitcast.1, s32[16]{0:T(128)} %order_in.1, bf16[512,512]{1,0:T(8,128)(2,1)} %w_in.1), custom_call_target="tpu_custom_call" | custom-call | tf_op jit(solution)/shard_map/pallas_call | solution.py:512
  47.9 1.9 %copy.8 = bf16[256,1024]{1,0:T(8,128)(2,1)} copy(bf16[256,1024]{1,0:T(8,128)(2,1)} %shard_map.64) | data formatting | bytes 1048576

commit v3 on v2

--- a/solution.py
+++ b/solution.py
@@ -90,7 +90,7 @@
 
 def line_kernel(
     n, q_in, k_in, v_in, doc_in, order_in, w_in, out_ref,
-    q_ref, doc_ref, order_ref, fetched, kbuf, vbuf, wbuf, bias, best, acc, att, far, stage, sums,
+    q_ref, doc_ref, order_ref, fetched, kbuf, vbuf, wbuf, bias, best, acc, att, far, stage,
     kv_send, kv_recv, w_send, w_recv, att_send, att_recv, far_send, far_recv, sum_send, sum_recv,
 ):
     seq, head = lax.axis_index("seq"), lax.axis_index("head")
@@ -218,6 +218,11 @@
     for fetch in fetches[2:]:
         fetch.wait()
 
+    def middle(who):
+        w_send_to(who, 1, 1, *parts[0])
+
+    each(lambda who: None, middle)
+
 
     down = lax.broadcasted_iota(jnp.int32, (span, span), 0)
     along = lax.broadcasted_iota(jnp.int32, (span, span), 1)
@@ -301,8 +306,7 @@
             kv_wait(which, 0, 3)
             kv_send_to(who, which, 1, 3)
             kv_send_to(who, which, 2, 3)
-        for cut, low in parts[:2]:
-            w_send_to(who, 1, 1, cut, low)
+        w_send_to(who, 1, 1, *parts[1])
         for cut, low in parts:
             w_send_to(who, 2, 1, cut, low)
 
@@ -362,12 +366,15 @@
     def _():
         att_near().start()
 
-    def att_wait():
-        arrive(att.at[1], att_recv.at[1])
-
-        @pl.when(jnp.logical_not(own_rows))
-        def _():
-            arrive(att.at[0], att_recv.at[0])
+    def far_copy(part):
+        return remote(att.at[part], far.at[part], far_send.at[part], far_recv.at[part], inward)
+
+    def own_far():
+        return remote(att.at[2], far.at[0], far_send.at[0], far_recv.at[0], inward)
+
+    @pl.when(own_rows & (role == 0))
+    def _():
+        own_far().start()
 
     def end(who):
         pass_w(who, 1, parts[:2], None)
@@ -379,23 +386,32 @@
             w_send_to(who, 1, 1, cut, low)
 
     each(end, middle)
-    att_wait()
-
-    def far_copy(part):
-        src = first_part if part == 0 else 1
-        return remote(att.at[src], far.at[part], far_send.at[part], far_recv.at[part], inward)
-
-    def end(who):
-        for part in range(2):
-            go(who, functools.partial(far_copy, part))
-
-    each(end, lambda who: None)
+
+    for part in (1 - c, c):
+
+        @pl.when(own_rows & (part == 1))
+        def _():
+            arrive(att.at[1], att_recv.at[1])
+
+        @pl.when(jnp.logical_not(own_rows))
+        def _(part=part):
+            arrive(att.at[part], att_recv.at[part])
+
+        @pl.when((role == 0) & (jnp.logical_not(own_rows) | (part == 1)))
+        def _(part=part):
+            far_copy(part).start()
+
+    def sum_at(row, lane, cut):
+        return out_ref.at[row, :, pl.ds(pl.multiple_of(lane * width + cut * half, half), half)]
 
     def sum_copy(k, slot, cut, zz):
         return remote(
-            stage.at[slot, cut], sums.at[y, x, cut], sum_send.at[slot, cut], sum_recv.at[y, x, cut],
+            stage.at[slot, cut], sum_at(y, x, cut), sum_send.at[slot, cut], sum_recv.at[y, x, cut],
             {"seq": 2 * zz + c, "head": slab(k)},
         )
+
+    def sum_stay(slot, cut):
+        return pltpu.make_async_copy(stage.at[slot, cut], sum_at(y, x, cut), sum_send.at[slot, cut])
 
     def here(k):
         return own_rows & (slab(k) == head)
@@ -407,13 +423,14 @@
     def project(k, slot, cut):
         value = product(k, cut, att[first_part], att[1]).astype(jnp.bfloat16)
 
+        stage[slot, cut] = value
+
         @pl.when(here(k))
         def _():
-            sums[y, x, cut] = value
+            sum_stay(slot, cut).start()
 
         @pl.when(jnp.logical_not(here(k)))
         def _():
-            stage[slot, cut] = value
             sum_copy(k, slot, cut, z).start()
 
     def project_far(who, cut):
@@ -471,18 +488,19 @@
 
                 @pl.when(jnp.logical_not(stays & (row == y) & (lane == x)))
                 def _():
-                    arrive(sums.at[row, lane, cut], sum_recv.at[row, lane, cut])
-
-            at = lane * width + cut * half
-            out_ref[:, at : at + half] = (
-                sums[0, lane, cut].astype(jnp.float32) + sums[1, lane, cut].astype(jnp.float32)
-            ).astype(jnp.bfloat16)
+                    arrive(sum_at(row, lane, cut), sum_recv.at[row, lane, cut])
 
     def finish(who):
         for make in sent[who]:
             make().wait_send()
 
     each(finish, finish)
+
+    @pl.when(role == 0)
+    def _():
+        for part in range(2):
+            far_copy(part).wait_send()
+
     att_cross().wait_send()
 
     @pl.when(jnp.logical_not(own_rows))
@@ -491,14 +509,17 @@
 
     for step in range(slabs):
         k = order[step]
-        made = jnp.logical_not(here(k))
-        if step == far_slab:
-            made = made & (role == 1)
-
-        @pl.when(made)
+        made = (role == 1) | (step != far_slab)
+
+        @pl.when(made & jnp.logical_not(here(k)))
         def _(k=k, step=step):
             for cut in cuts:
                 sum_copy(k, step, cut, z).wait_send()
+
+        @pl.when(made & here(k))
+        def _(step=step):
+            for cut in cuts:
+                sum_stay(step, cut).wait()
 
 
 def line_form(n, queries, keys, values, doc_ids, span_order, out_weight):
@@ -509,11 +530,11 @@
     heads = queries.shape[1] // DH
     bf16 = jnp.bfloat16
     dma = pltpu.SemaphoreType.DMA
-    return pl.pallas_call(
+    sums = pl.pallas_call(
         functools.partial(line_kernel, n),
-        out_shape=jax.ShapeDtypeStruct((rows, 2 * width), bf16),
+        out_shape=jax.ShapeDtypeStruct((2, rows, 2 * width), bf16),
         in_specs=[pl.BlockSpec(memory_space=pl.ANY)] * 6,
-        out_specs=pl.BlockSpec(memory_space=pltpu.VMEM),
+        out_specs=pl.BlockSpec(memory_space=pl.ANY),
         scratch_shapes=[
             pltpu.VMEM(queries.shape, bf16),
             pltpu.VMEM((doc_ids.shape[0] // (rows // 2), rows // 2), jnp.int32),
@@ -528,7 +549,6 @@
             pltpu.VMEM((3,) + queries.shape, bf16),
             pltpu.VMEM((2,) + queries.shape, bf16),
             pltpu.VMEM((slabs + 1, 2, rows, half), bf16),
-            pltpu.VMEM((2, 2, 2, rows, half), bf16),
             dma((2, 3, slabs)),
             dma((2, 2, slabs)),
             dma((3, slabs, 2, 2)),
@@ -544,6 +564,7 @@
             collective_id=0, has_side_effects=True, vmem_limit_bytes=62 * 1024 * 1024
         ),
     )(queries, keys, values, doc_ids.reshape(-1, rows // 2), span_order, out_weight)
+    return (sums[0].astype(jnp.float32) + sums[1].astype(jnp.float32)).astype(bf16)
 
 
 def on_device(mesh_shape, queries, keys, values, doc_ids, span_order, out_weight):

time: 50.4 us -> 47.6 us (0.944)
  the two profiles are of different devices: /device:TPU:0 before, /device:TPU:25 now
where the time goes in v3:
time: 47.6 us; the launch traced here: 47.5 us
  Pallas kernels  45.3 us (95%)
  other arithmetic  2.19 us (5%)
    pallas_call x1, Pallas kernels, line_form(): pl.pallas_call(functools.partial(line_kernel, n), out_shape=jax.ShapeDtyp...  45.3 us
    convert_element_type x1, other arithmetic, line_form(): (sums[0].astype(jnp.float32) + sums[1].astype(jnp.float32)).astype(bf16)  2.19 us

profile of v3, /device:TPU:25, one launch (start us, length us, event | category | flops | bytes accessed | tf_op | source)
XLA Modules:
  0.0 47.5 jit_solution(3421488440559939243)
XLA Ops:
  0.0 45.3 %shard_map.64 = bf16[2,256,1024]{2,1,0:T(8,128)(2,1)} custom-call(bf16[256,512]{1,0:T(8,128)(2,1)} %q_in.1, bf16[256,128]{1,0:T(8,128)(2,1)} %k_in.1, bf16[256,128]{1,0:T(8,128)(2,1)} %v_in.1, s32[16,128]{1,0:T(8,128)} %bitcast.3, s32[16]{0:T(128)} %order_in.1, bf16[512,512]{1,0:T(8,128)(2,1)} %w_in.1), custom_call_target="tpu_custom_call" | custom-call | tf_op jit(solution)/shard_map/pallas_call | solution.py:533
  45.3 2.2 %fusion = bf16[256,1024]{1,0:T(8,128)(2,1)} fusion(bf16[2,256,1024]{2,1,0:T(8,128)(2,1)} %shard_map.64), kind=kLoop, calls=%fused_computation.1 | loop fusion | flops 1048576 | bytes 1572864 | tf_op jit(solution)/shard_map/convert_element_type | solution.py:567

commit v4 on v3

--- a/solution.py
+++ b/solution.py
@@ -125,10 +125,7 @@
         pltpu.make_async_copy(src, dst, fetched.at[at])
         for at, (src, dst) in enumerate(
             [(k_in, kbuf.at[own, 0]), (v_in, vbuf.at[own, 0])]
-            + [
-                (w_in.at[pl.ds(low * deep, deep), pl.ds(cut * half, half)], wbuf.at[own, cut, pl.ds(low * deep, deep)])
-                for cut, low in parts
-            ]
+            + [(w_in.at[:, pl.ds(cut * half, half)], wbuf.at[own, cut, pl.ds(0, depth)]) for cut in range(2)]
             + [(doc_in, doc_ref), (order_in, order_ref), (q_in, q_ref)]
         )
     ]
@@ -154,11 +151,7 @@
             src_ref=src, dst_ref=dst, send_sem=send, recv_sem=recv, device_id=device, device_id_type=MESH
         )
 
-    sent = ([], [])
-
-    def go(who, make):
-        make().start()
-        sent[who].append(make)
+    passed, pieces = [0, 0], [0, 0]
 
     def arrive(dst, recv):
         remote(dst, dst, att_send.at[0], recv, partner).wait_recv()
@@ -167,15 +160,16 @@
         buf = (kbuf, vbuf)[which]
         to = slabs - 1 - k if (who == 1 and way == 0) else k
         lane = 1 if way == 2 else 0
-        go(
-            who,
-            lambda: remote(
-                buf.at[k, 0], buf.at[to, lane], kv_send.at[which, way, k], kv_recv.at[which, lane, to], ways[way]
-            ),
-        )
-
-    def kv_wait(which, lane, k):
-        arrive((kbuf, vbuf)[which].at[k, lane], kv_recv.at[which, lane, k])
+        at = which if lane == 0 else 2
+        remote(buf.at[k, 0], buf.at[to, lane], kv_send, kv_recv.at[at, to], ways[way]).start()
+        passed[who] += 1
+
+    def kv_wait(which, k):
+        arrive((kbuf, vbuf)[which].at[k, 0], kv_recv.at[which, k])
+
+    def kv_pair_wait(k):
+        both = q_ref.at[:, pl.ds(0, 2 * DH)]
+        arrive(both, kv_recv.at[2, k])
 
     def w_at(k, cut, low, mine):
         return wbuf.at[k, cut, pl.ds(mine * depth + low * deep, deep)]
@@ -183,16 +177,14 @@
     def w_send_to(who, way, k, cut, low):
         to = slabs - 1 - k if (who == 1 and way == 0) else k
         mine = 1 if way == 2 else 0
-        go(
-            who,
-            lambda: remote(
-                w_at(k, cut, low, 0), w_at(to, cut, low, mine), w_send.at[way, k, cut, low],
-                w_recv.at[mine, to, cut, low], partner if way == 2 else ways[way],
-            ),
-        )
-
-    def w_wait(mine, k, cut, low):
-        arrive(w_at(k, cut, low, mine), w_recv.at[mine, k, cut, low])
+        remote(
+            w_at(k, cut, low, 0), w_at(to, cut, low, mine), w_send, w_recv.at[mine, to, cut, 0 if mine else low],
+            partner if way == 2 else ways[way],
+        ).start()
+        pieces[who] += 1
+
+    def w_wait(k, cut, low):
+        arrive(w_at(k, cut, low, 0), w_recv.at[0, k, cut, low])
 
     def each(end, middle):
         @pl.when(role == 0)
@@ -276,8 +268,7 @@
             att[2, :, h * DH : (h + 1) * DH] = (summed[:, :DH] / summed[:, DH:]).astype(jnp.bfloat16)
 
     def group(step):
-        for which in range(2):
-            kv_wait(which, 1, order[step])
+        kv_pair_wait(order[step])
         for h in range(heads):
             attend(step, h)
 
@@ -285,7 +276,7 @@
 
     def end(who):
         for which in range(2):
-            kv_wait(which, 0, 1)
+            kv_wait(which, 1)
             kv_send_to(who, which, 2, 1)
         for cut, low in parts:
             w_send_to(who, 0, 0, cut, low)
@@ -294,16 +285,16 @@
 
     def middle(who):
         for which in range(2):
-            kv_wait(which, 0, 0)
+            kv_wait(which, 0)
             kv_send_to(who, which, 0, 0)
             kv_send_to(who, which, 2, 0)
-            kv_wait(which, 0, 2)
+            kv_wait(which, 2)
             kv_send_to(who, which, 1, 2)
             kv_send_to(who, which, 2, 2)
         for cut, low in parts:
             w_send_to(who, 0, 1, cut, low)
         for which in range(2):
-            kv_wait(which, 0, 3)
+            kv_wait(which, 3)
             kv_send_to(who, which, 1, 3)
             kv_send_to(who, which, 2, 3)
         w_send_to(who, 1, 1, *parts[1])
@@ -316,7 +307,7 @@
 
     def end(who):
         for which in range(2):
-            kv_wait(which, 0, 2)
+            kv_wait(which, 2)
             kv_send_to(who, which, 2, 2)
 
     each(end, lambda who: None)
@@ -326,14 +317,14 @@
 
     def pass_w(who, k, which, way):
         for cut, low in which:
-            w_wait(0, k, cut, low)
+            w_wait(k, cut, low)
             if way is not None:
                 w_send_to(who, way, k, cut, low)
             w_send_to(who, 2, k, cut, low)
 
     def end(who):
         for which in range(2):
-            kv_wait(which, 0, 3)
+            kv_wait(which, 3)
             kv_send_to(who, which, 2, 3)
 
     def middle(who):
@@ -367,10 +358,10 @@
         att_near().start()
 
     def far_copy(part):
-        return remote(att.at[part], far.at[part], far_send.at[part], far_recv.at[part], inward)
+        return remote(att.at[part], far.at[part], far_send, far_recv, inward)
 
     def own_far():
-        return remote(att.at[2], far.at[0], far_send.at[0], far_recv.at[0], inward)
+        return remote(att.at[2], far.at[0], far_send, far_recv, inward)
 
     @pl.when(own_rows & (role == 0))
     def _():
@@ -406,12 +397,12 @@
 
     def sum_copy(k, slot, cut, zz):
         return remote(
-            stage.at[slot, cut], sum_at(y, x, cut), sum_send.at[slot, cut], sum_recv.at[y, x, cut],
+            stage.at[slot, cut], sum_at(y, x, cut), sum_send, sum_recv,
             {"seq": 2 * zz + c, "head": slab(k)},
         )
 
     def sum_stay(slot, cut):
-        return pltpu.make_async_copy(stage.at[slot, cut], sum_at(y, x, cut), sum_send.at[slot, cut])
+        return pltpu.make_async_copy(stage.at[slot, cut], sum_at(y, x, cut), sum_recv)
 
     def here(k):
         return own_rows & (slab(k) == head)
@@ -435,11 +426,10 @@
 
     def project_far(who, cut):
         stage[slabs, cut] = product(far_slab, cut, far[0], far[1]).astype(jnp.bfloat16)
-        go(who, lambda: sum_copy(far_slab, slabs, cut, slab(0)))
+        sum_copy(far_slab, slabs, cut, slab(0)).start()
 
     def near_w(k, cut):
-        for low in range(2):
-            w_wait(1, k, cut, low)
+        arrive(wbuf.at[k, cut, pl.ds(depth, depth)], w_recv.at[1, k, cut, 0])
 
     for cut in cuts:
         near_w(order[0], cut)
@@ -472,8 +462,7 @@
         near_w(3, 0)
         project(3, 3, 0)
         pass_w(who, 3, parts[2:], None)
-        for part in range(2):
-            arrive(far.at[part], far_recv.at[part])
+        arrive(far, far_recv)
         project_far(who, 0)
         near_w(3, 1)
         project_far(who, 1)
@@ -482,44 +471,35 @@
     each(end, middle)
 
     stays = own_rows & ((role == 1) | (slab(far_slab) != head))
-    for cut in cuts:
-        for lane in range(2):
-            for row in range(2):
-
-                @pl.when(jnp.logical_not(stays & (row == y) & (lane == x)))
-                def _():
-                    arrive(sum_at(row, lane, cut), sum_recv.at[row, lane, cut])
+
+    def left(ref, send):
+        remote(ref, ref, send, sum_recv, partner).wait_send()
 
     def finish(who):
-        for make in sent[who]:
-            make().wait_send()
-
-    each(finish, finish)
-
-    @pl.when(role == 0)
-    def _():
-        for part in range(2):
-            far_copy(part).wait_send()
-
+        left(wbuf.at[:2, :, pl.ds(0, passed[who] * rows * DH // (4 * half))], kv_send)
+        left(wbuf.at[: pieces[who] // (2 * len(parts))], w_send)
+        made = 2 * slabs + 2 if who == 1 else 2 * slabs - 2
+
+        @pl.when(stays)
+        def _():
+            left(stage.at[: made // 2 - 1], sum_send)
+
+        @pl.when(jnp.logical_not(stays))
+        def _():
+            left(stage.at[: made // 2], sum_send)
+
+    def end(who):
+        left(far, far_send)
+        finish(who)
+
+    each(end, finish)
     att_cross().wait_send()
 
     @pl.when(jnp.logical_not(own_rows))
     def _():
         att_near().wait_send()
 
-    for step in range(slabs):
-        k = order[step]
-        made = (role == 1) | (step != far_slab)
-
-        @pl.when(made & jnp.logical_not(here(k)))
-        def _(k=k, step=step):
-            for cut in cuts:
-                sum_copy(k, step, cut, z).wait_send()
-
-        @pl.when(made & here(k))
-        def _(step=step):
-            for cut in cuts:
-                sum_stay(step, cut).wait()
+    arrive(out_ref, sum_recv)
 
 
 def line_form(n, queries, keys, values, doc_ids, span_order, out_weight):
@@ -539,7 +519,7 @@
             pltpu.VMEM(queries.shape, bf16),
             pltpu.VMEM((doc_ids.shape[0] // (rows // 2), rows // 2), jnp.int32),
             pltpu.SMEM(span_order.shape, jnp.int32),
-            dma((9,)),
+            dma((7,)),
             pltpu.VMEM((slabs, 2, rows, DH), bf16),
             pltpu.VMEM((slabs, 2, rows, DH), bf16),
             pltpu.VMEM((slabs, 2, 2 * depth, half), bf16),
@@ -549,16 +529,16 @@
             pltpu.VMEM((3,) + queries.shape, bf16),
             pltpu.VMEM((2,) + queries.shape, bf16),
             pltpu.VMEM((slabs + 1, 2, rows, half), bf16),
-            dma((2, 3, slabs)),
-            dma((2, 2, slabs)),
-            dma((3, slabs, 2, 2)),
+            dma,
+            dma((3, slabs)),
+            dma,
             dma((2, slabs, 2, 2)),
             dma((2,)),
             dma((2,)),
-            dma((2,)),
-            dma((2,)),
-            dma((slabs + 1, 2)),
-            dma((2, 2, 2)),
+            dma,
+            dma,
+            dma,
+            dma,
         ],
         compiler_params=pltpu.CompilerParams(
             collective_id=0, has_side_effects=True, vmem_limit_bytes=62 * 1024 * 1024

time: 47.6 us -> 46.6 us (0.979)
  Pallas kernels: 45.3 us -> 44.3 us
    pallas_call x1, Pallas kernels: 45.3 us -> 44.3 us  [line_form(): pl.pallas_call(functools.partial(line_kernel, n), out_shape=jax.ShapeDtyp...]
where the time goes in v4:
time: 46.6 us; the launch traced here: 46.5 us
  Pallas kernels  44.3 us (95%)
  other arithmetic  2.19 us (5%)
    pallas_call x1, Pallas kernels, line_form(): pl.pallas_call(functools.partial(line_kernel, n), out_shape=jax.ShapeDtyp...  44.3 us
    convert_element_type x1, other arithmetic, line_form(): (sums[0].astype(jnp.float32) + sums[1].astype(jnp.float32)).astype(bf16)  2.19 us

profile of v4, /device:TPU:25, one launch (start us, length us, event | category | flops | bytes accessed | tf_op | source)
XLA Modules:
  0.0 46.5 jit_solution(8564079320839241326)
XLA Ops:
  0.0 44.3 %shard_map.64 = bf16[2,256,1024]{2,1,0:T(8,128)(2,1)} custom-call(bf16[256,512]{1,0:T(8,128)(2,1)} %q_in.1, bf16[256,128]{1,0:T(8,128)(2,1)} %k_in.1, bf16[256,128]{1,0:T(8,128)(2,1)} %v_in.1, s32[16,128]{1,0:T(8,128)} %bitcast.3, s32[16]{0:T(128)} %order_in.1, bf16[512,512]{1,0:T(8,128)(2,1)} %w_in.1), custom_call_target="tpu_custom_call" | custom-call | tf_op jit(solution)/shard_map/pallas_call | solution.py:513
  44.3 2.2 %fusion = bf16[256,1024]{1,0:T(8,128)(2,1)} fusion(bf16[2,256,1024]{2,1,0:T(8,128)(2,1)} %shard_map.64), kind=kLoop, calls=%fused_computation.1 | loop fusion | flops 1048576 | bytes 1572864 | tf_op jit(solution)/shard_map/convert_element_type | solution.py:547

commit v5 on v4

--- a/solution.py
+++ b/solution.py
@@ -133,18 +133,15 @@
         fetch.start()
 
     barrier = pltpu.get_barrier_semaphore()
-    for zz in range(2):
-        for flip in range(8):
-            fx, fy, fc = flip // 4, flip // 2 % 2, flip % 2
-            if zz or flip:
-                there = place((z - 2 * side + zz) % 2 + 2 * side, (x + fx) % 2, (y + fy) % 2, (c + fc) % 2)
-                pl.semaphore_signal(barrier, inc=1, device_id=there, device_id_type=MESH)
+    nearby = place((1 - role) * slab(1) + role * slab(0), x, y, c)
+    for there in (nearby, across, partner, {"head": 2 * (1 - y) + c}):
+        pl.semaphore_signal(barrier, inc=1, device_id=there, device_id_type=MESH)
 
     @pl.when(role == 1)
     def _():
         pl.semaphore_signal(barrier, inc=1, device_id=inward, device_id_type=MESH)
 
-    pl.semaphore_wait(barrier, 15 + role)
+    pl.semaphore_wait(barrier, 4 + role)
 
     def remote(src, dst, send, recv, device):
         return pltpu.make_async_remote_copy(
@@ -500,6 +497,44 @@
         att_near().wait_send()
 
     arrive(out_ref, sum_recv)
+
+
+def add_kernel(pair_in, out, pair, total, came, went):
+    pieces = pair.shape[0]
+    rows = pair.shape[2]
+
+    def fetch(at):
+        return pltpu.make_async_copy(pair_in.at[:, pl.ds(at * rows, rows)], pair.at[at], came.at[at])
+
+    def leave(at):
+        return pltpu.make_async_copy(total.at[at], out.at[pl.ds(at * rows, rows)], went.at[at])
+
+    for at in range(pieces):
+        fetch(at).start()
+    for at in range(pieces):
+        fetch(at).wait()
+        total[at] = (pair[at, 0].astype(jnp.float32) + pair[at, 1].astype(jnp.float32)).astype(total.dtype)
+        leave(at).start()
+    for at in range(pieces):
+        leave(at).wait()
+
+
+def add_form(sums):
+    pieces = 4
+    rows, columns = sums.shape[1] // pieces, sums.shape[2]
+    return pl.pallas_call(
+        add_kernel,
+        out_shape=jax.ShapeDtypeStruct(sums.shape[1:], sums.dtype),
+        in_specs=[pl.BlockSpec(memory_space=pl.ANY)],
+        out_specs=pl.BlockSpec(memory_space=pl.ANY),
+        scratch_shapes=[
+            pltpu.VMEM((pieces, 2, rows, columns), sums.dtype),
+            pltpu.VMEM((pieces, rows, columns), sums.dtype),
+            pltpu.SemaphoreType.DMA((pieces,)),
+            pltpu.SemaphoreType.DMA((pieces,)),
+        ],
+        compiler_params=pltpu.CompilerParams(vmem_limit_bytes=62 * 1024 * 1024),
+    )(sums)
 
 
 def line_form(n, queries, keys, values, doc_ids, span_order, out_weight):
@@ -544,7 +579,7 @@
             collective_id=0, has_side_effects=True, vmem_limit_bytes=62 * 1024 * 1024
         ),
     )(queries, keys, values, doc_ids.reshape(-1, rows // 2), span_order, out_weight)
-    return (sums[0].astype(jnp.float32) + sums[1].astype(jnp.float32)).astype(bf16)
+    return add_form(sums)
 
 
 def on_device(mesh_shape, queries, keys, values, doc_ids, span_order, out_weight):

time: 46.6 us -> 46.2 us (level)
  the two profiles are of different devices: /device:TPU:25 before, /device:TPU:0 now
where the time goes in v5:
time: 46.2 us; the launch traced here: 45.4 us
  Pallas kernels  45.4 us (98%)
    pallas_call x1, Pallas kernels, line_form(): pl.pallas_call(functools.partial(line_kernel, n), out_shape=jax.ShapeDtyp...  43.5 us
    pallas_call x1, Pallas kernels, add_form(): pl.pallas_call(add_kernel, out_shape=jax.ShapeDtypeStruct(sums.shape[1:],...  1.94 us

profile of v5, /device:TPU:0, one launch (start us, length us, event | category | flops | bytes accessed | tf_op | source)
XLA Modules:
  0.0 45.4 jit_solution(6311416606624382687)
XLA Ops:
  0.0 43.5 %shard_map.64.pair_in = bf16[2,256,1024]{2,1,0:T(8,128)(2,1)} custom-call(bf16[256,512]{1,0:T(8,128)(2,1)} %q_in.1, bf16[256,128]{1,0:T(8,128)(2,1)} %k_in.1, bf16[256,128]{1,0:T(8,128)(2,1)} %v_in.1, s32[16,128]{1,0:T(8,128)} %bitcast.1, s32[16]{0:T(128)} %order_in.1, bf16[512,512]{1,0:T(8,128)(2,1)} %w_in.1), custom_call_target="tpu_custom_call" | custom-call | tf_op jit(solution)/shard_map/pallas_call | solution.py:548
  43.5 1.9 %shard_map.65 = bf16[256,1024]{1,0:T(8,128)(2,1)} custom-call(bf16[2,256,1024]{2,1,0:T(8,128)(2,1)} %shard_map.64.pair_in), custom_call_target="tpu_custom_call" | custom-call | tf_op jit(solution)/shard_map/pallas_call | solution.py:525

commit v6 on v5

--- a/solution.py
+++ b/solution.py
@@ -104,7 +104,7 @@
     half, deep = width // 2, depth // 2
     factor = math.log2(math.e) / math.sqrt(DH)
     slabs = n // 2
-    far_slab = slabs - 1
+    handed = ((1, 1), (slabs - 1, 0), (slabs - 1, 1))
     cuts = range(2)
     parts = [(cut, low) for cut in range(2) for low in range(2)]
 
@@ -348,34 +348,32 @@
     def att_near():
         return remote(att.at[2], att.at[1], att_send.at[1], att_recv.at[1], partner)
 
+
+    def far_copy(flip):
+        there = place(slab(1), (x + flip) % 2, y, x)
+        return remote(att.at[2], far.at[cross_part], far_send, far_recv, there)
+
+    @pl.when(role == 0)
+    def _():
+        for flip in range(2):
+            far_copy(flip).start()
+
     att_cross().start()
 
     @pl.when(jnp.logical_not(own_rows))
     def _():
         att_near().start()
 
-    def far_copy(part):
-        return remote(att.at[part], far.at[part], far_send, far_recv, inward)
-
-    def own_far():
-        return remote(att.at[2], far.at[0], far_send, far_recv, inward)
-
-    @pl.when(own_rows & (role == 0))
-    def _():
-        own_far().start()
-
     def end(who):
         pass_w(who, 1, parts[:2], None)
 
     def middle(who):
         pass_w(who, 0, parts[2:], 0)
         pass_w(who, 2, parts[2:], 1)
-        for cut, low in parts[2:]:
-            w_send_to(who, 1, 1, cut, low)
 
     each(end, middle)
 
-    for part in (1 - c, c):
+    for turn, part in enumerate((1 - c, c)):
 
         @pl.when(own_rows & (part == 1))
         def _():
@@ -385,16 +383,15 @@
         def _(part=part):
             arrive(att.at[part], att_recv.at[part])
 
-        @pl.when((role == 0) & (jnp.logical_not(own_rows) | (part == 1)))
-        def _(part=part):
-            far_copy(part).start()
+        if turn == 0:
+            each(lambda who: pass_w(who, 2, parts[:2], None), lambda who: None)
 
     def sum_at(row, lane, cut):
         return out_ref.at[row, :, pl.ds(pl.multiple_of(lane * width + cut * half, half), half)]
 
-    def sum_copy(k, slot, cut, zz):
+    def sum_copy(k, slot, at, zz, cut):
         return remote(
-            stage.at[slot, cut], sum_at(y, x, cut), sum_send, sum_recv,
+            stage.at[slot, at], sum_at(y, x, cut), sum_send, sum_recv,
             {"seq": 2 * zz + c, "head": slab(k)},
         )
 
@@ -419,19 +416,22 @@
 
         @pl.when(jnp.logical_not(here(k)))
         def _():
-            sum_copy(k, slot, cut, z).start()
-
-    def project_far(who, cut):
-        stage[slabs, cut] = product(far_slab, cut, far[0], far[1]).astype(jnp.bfloat16)
-        sum_copy(far_slab, slabs, cut, slab(0)).start()
+            sum_copy(k, slot, cut, z, cut).start()
+
+    def project_far(at):
+        k, cut = handed[at]
+        slot, lane = slabs + at // 2, at % 2
+        stage[slot, lane] = product(k, cut, far[0], far[1]).astype(jnp.bfloat16)
+        sum_copy(k, slot, lane, slab(0), cut).start()
 
     def near_w(k, cut):
         arrive(wbuf.at[k, cut, pl.ds(depth, depth)], w_recv.at[1, k, cut, 0])
 
+    near_w(2, 0)
+    project(2, 2, 0)
     for cut in cuts:
         near_w(order[0], cut)
         project(order[0], 0, cut)
-
     near_w(order[1], 0)
     project(order[1], 1, 0)
 
@@ -440,50 +440,44 @@
         project(0, 1, 1)
 
     each(lambda who: None, middle)
-    for cut in cuts:
-
-        def end(who):
-            pass_w(who, 2, [(cut, low) for low in range(2)], None)
-
-        each(end, lambda who: None)
-        near_w(2, cut)
-        project(2, 2, cut)
-
-    def end(who):
-        pass_w(who, 1, parts[2:], None)
-        near_w(1, 1)
-        project(1, 1, 1)
+    each(lambda who: pass_w(who, 2, parts[2:], None), lambda who: None)
+    near_w(2, 1)
+    project(2, 2, 1)
 
     def middle(who):
         pass_w(who, 3, parts[:2], None)
         near_w(3, 0)
         project(3, 3, 0)
-        pass_w(who, 3, parts[2:], None)
+        pass_w(who, 3, parts[2:3], None)
         arrive(far, far_recv)
-        project_far(who, 0)
+        project_far(0)
+        project_far(1)
+        pass_w(who, 3, parts[3:], None)
         near_w(3, 1)
-        project_far(who, 1)
+        project_far(2)
         project(3, 3, 1)
 
-    each(end, middle)
-
-    stays = own_rows & ((role == 1) | (slab(far_slab) != head))
+    each(lambda who: None, middle)
 
     def left(ref, send):
         remote(ref, ref, send, sum_recv, partner).wait_send()
 
     def finish(who):
         left(wbuf.at[:2, :, pl.ds(0, passed[who] * rows * DH // (4 * half))], kv_send)
-        left(wbuf.at[: pieces[who] // (2 * len(parts))], w_send)
-        made = 2 * slabs + 2 if who == 1 else 2 * slabs - 2
-
-        @pl.when(stays)
-        def _():
-            left(stage.at[: made // 2 - 1], sum_send)
-
-        @pl.when(jnp.logical_not(stays))
-        def _():
-            left(stage.at[: made // 2], sum_send)
+        left(wbuf.at[:, :, pl.ds(0, pieces[who] * deep // (2 * slabs))], w_send)
+        full = 2 * slabs + len(handed) if who == 1 else 2 * slabs - len(handed)
+        kept = [len([1 for cut in cuts if who == 1 or (k, cut) not in handed]) for k in range(slabs)]
+        for count in range(3):
+            mine = [slab(k) == head for k in range(slabs) if kept[k] == count]
+            if count == 0:
+                mine.append(jnp.logical_not(own_rows))
+            if mine:
+                held = functools.reduce(jnp.logical_or, mine)
+                held = held if count == 0 else held & own_rows
+
+                @pl.when(held)
+                def _(count=count):
+                    left(wbuf.at[:2, :, pl.ds(0, (full - count) * rows // 4)], sum_send)
 
     def end(who):
         left(far, far_send)
@@ -563,7 +557,7 @@
             pltpu.VMEM((heads, rows, 2 * DH), jnp.float32),
             pltpu.VMEM((3,) + queries.shape, bf16),
             pltpu.VMEM((2,) + queries.shape, bf16),
-            pltpu.VMEM((slabs + 1, 2, rows, half), bf16),
+            pltpu.VMEM((slabs + 2, 2, rows, half), bf16),
             dma,
             dma((3, slabs)),
             dma,

time: 46.2 us -> 46.1 us (level)
  the two profiles are of different devices: /device:TPU:0 before, /device:TPU:5 now
where the time goes in v6:
time: 46.1 us; the launch traced here: 46 us
  Pallas kernels  46 us (100%)
    pallas_call x1, Pallas kernels, line_form(): pl.pallas_call(functools.partial(line_kernel, n), out_shape=jax.ShapeDtyp...  44 us
    pallas_call x1, Pallas kernels, add_form(): pl.pallas_call(add_kernel, out_shape=jax.ShapeDtypeStruct(sums.shape[1:],...  1.94 us

profile of v6, /device:TPU:5, one launch (start us, length us, event | category | flops | bytes accessed | tf_op | source)
XLA Modules:
  0.0 46.0 jit_solution(6850943074564347013)
XLA Ops:
  0.0 44.0 %shard_map.64.pair_in = bf16[2,256,1024]{2,1,0:T(8,128)(2,1)} custom-call(bf16[256,512]{1,0:T(8,128)(2,1)} %q_in.1, bf16[256,128]{1,0:T(8,128)(2,1)} %k_in.1, bf16[256,128]{1,0:T(8,128)(2,1)} %v_in.1, s32[16,128]{1,0:T(8,128)} %bitcast.1, s32[16]{0:T(128)} %order_in.1, bf16[512,512]{1,0:T(8,128)(2,1)} %w_in.1), custom_call_target="tpu_custom_call" | custom-call | tf_op jit(solution)/shard_map/pallas_call | solution.py:542
  44.0 1.9 %shard_map.65 = bf16[256,1024]{1,0:T(8,128)(2,1)} custom-call(bf16[2,256,1024]{2,1,0:T(8,128)(2,1)} %shard_map.64.pair_in), custom_call_target="tpu_custom_call" | custom-call | tf_op jit(solution)/shard_map/pallas_call | solution.py:519
